TPU v7x, 32 devices: a whole 2x2x4 slice. The times are simulated.
32 devices in a mesh: mem: 8 (over y, x, core), tile: 4 (over z).
Axes of the slice: x: 2, y: 2, z: 4, core: 2. Of those that a mesh axis runs over, the one named last changes fastest.
Arguments:
- perturbations: bfloat16 [16, 4, 128, 1024], P('mem', None, 'tile'), may hold values from -6 to 6
- right_side: float32 [4, 128, 1024], P(None, 'tile'), may hold values from -14 to 14
- fine_taps: float32 [2, 4, 5], replicated, may hold values from 0.3 to 1
- coarse_lat: float32 [32, 32], replicated, may hold values from -4 to 16, as said below
- coarse_lon: float32 [256, 256], replicated, may hold values from -4 to 16, as said below
Outputs:
- solution: float32 [4, 128, 1024], P(None, 'tile', 'mem')
- residual: float32 [4, 128, 1024], P(None, 'tile', 'mem')
Inputs may be any that keep to these rules, and one draw needn't show every extreme that they name: `coarse_lat`: symmetric. `coarse_lon`: symmetric.
All inputs are finite; a program needn't handle non-finite values.
Results may differ from a plain program's by a relative error of at most 0.0003.
Values may be sent and summed in bfloat16 or wider, within the bound.
A program may use at most 64 MiB of HBM per device.

v0:
```python
import jax
import jax.numpy as jnp
from jax import lax
from jax.sharding import PartitionSpec as P

ITERS = 2
exact_mode = lax.Precision.HIGHEST


def extended_2(array, sides, width):
    for axis, dim in sides:
        peers, length = (lax.axis_size(axis), array.shape[dim])
        up = [(i, (i + 1) % peers) for i in range(peers - 1)]
        down = [(j, i) for i, j in up]
        last = lax.slice_in_dim(array, length - width, length, axis=dim)
        first = lax.slice_in_dim(array, 0, width, axis=dim)
        before = lax.ppermute(last, axis, up)
        after = lax.ppermute(first, axis, down)
        array = jnp.concatenate([before, array, after], axis=dim)
    return array


def normalized(fine_taps):
    energy = fine_taps[:, :, 0] ** 2 + 2.0 * jnp.sum(fine_taps[:, :, 1:] ** 2, axis=2)
    return fine_taps / jnp.sqrt(energy)[:, :, None]


def lat_valid(values, kernel, height):
    result = kernel[None, :, 0, None, None] * values[:, :, 4 : 4 + height]
    for offset in range(1, 5):
        result = result + kernel[None, :, offset, None, None] * (
            values[:, :, 4 + offset : 4 + offset + height]
            + values[:, :, 4 - offset : 4 - offset + height]
        )
    return result


def lon_pass(values, kernel):
    result = kernel[None, :, 0, None, None] * values
    for offset in range(1, 5):
        result = result + kernel[None, :, offset, None, None] * (
            jnp.roll(values, offset, axis=3) + jnp.roll(values, -offset, axis=3)
        )
    return result


def shrink_table(extent):
    fine_index = jnp.arange(extent)[:, None] // 4
    coarse_index = jnp.arange(extent // 4)[None, :]
    return (fine_index == coarse_index).astype(jnp.float32) * 0.25


def expand_table(extent):
    coarse_index = jnp.arange(extent // 4)[:, None]
    fine_index = jnp.arange(extent)[None, :] // 4
    return (fine_index == coarse_index).astype(jnp.float32)


def block_mean(values):
    shape_now = values.shape
    lat_mean = (
        jnp.sum(
            values.reshape(shape_now[0], shape_now[1], shape_now[2] // 4, 4, shape_now[3]), axis=3
        )
        * 0.25
    )
    return jnp.einsum("abcd,de->abce", lat_mean, shrink_table(shape_now[3]), precision=exact_mode)


def prolong(coarse):
    shape_now = coarse.shape
    extent = shape_now[3] * 4
    widened = jnp.einsum("abce,ed->abcd", coarse, expand_table(extent), precision=exact_mode)
    spread_out = jnp.broadcast_to(
        widened[:, :, :, None, :], (shape_now[0], shape_now[1], shape_now[2], 4, extent)
    )
    return spread_out.reshape(shape_now[0], shape_now[1], shape_now[2] * 4, extent)


def local(perturbations, right_side, fine_taps, coarse_lat, coarse_lon):
    kernel = normalized(fine_taps)
    count_local, levels, height, extent = perturbations.shape
    groups = lax.axis_size("mem")
    members = count_local * groups
    share_width = extent // groups
    share_start = lax.axis_index("mem") * share_width
    tile_count = lax.axis_size("tile")
    residual_full = right_side
    residual = lax.dynamic_slice_in_dim(right_side, share_start, share_width, 2)
    solution = jnp.zeros_like(residual)
    squares = lax.psum(jnp.sum(residual * residual), ("mem", "tile"))
    for iteration in range(ITERS):
        weighted = perturbations.astype(jnp.float32) * residual_full[None]
        coarse = block_mean(weighted)
        apply_detail = weighted - prolong(coarse)
        coarse_items = coarse.reshape(
            tile_count, count_local * levels // tile_count, height // 4, extent // 4
        )
        across = jnp.einsum(
            "ab,skbc->skac",
            coarse_lat,
            lax.all_to_all(coarse_items, "tile", split_axis=0, concat_axis=2, tiled=True),
            precision=exact_mode,
        )
        smoothed = jnp.einsum("skac,cd->skad", across, coarse_lon, precision=exact_mode)
        detail = apply_detail
        for repeat in range(2):
            extended = extended_2(detail, (("tile", 2),), 4)
            detail = lat_valid(extended, kernel[0], height)
        apply_detail = detail
        apply_detail = lon_pass(lon_pass(apply_detail, kernel[1]), kernel[1])
        returned = lax.all_to_all(
            smoothed, "tile", split_axis=2, concat_axis=0, tiled=True
        ).reshape(count_local, levels, height // 4, extent // 4)
        blended = apply_detail - prolong(block_mean(apply_detail)) + prolong(returned)
        partial_value = jnp.sum(perturbations.astype(jnp.float32) * blended, axis=0)
        applied = residual + lax.psum_scatter(
            partial_value, "mem", scatter_dimension=2, tiled=True
        ) / (members - 1)
        step_size = squares / lax.psum(jnp.sum(residual * applied), ("mem", "tile"))
        solution = solution + step_size * residual
        residual = residual - step_size * applied
        if iteration + 1 < ITERS:
            squares = lax.psum(jnp.sum(residual * residual), ("mem", "tile"))
            residual_full = lax.all_gather(residual, "mem", axis=2, tiled=True)
    return (solution, residual)


def solution(mesh):
    placed = (P("mem", None, "tile", None), P(None, "tile", None), P(), P(), P())
    return jax.shard_map(
        local,
        mesh=mesh,
        in_specs=placed,
        out_specs=(P(None, "tile", "mem"), P(None, "tile", "mem")),
        check_vma=False,
    )
```

profile of v0, /device:TPU:0, one launch (start us, length us, event | category | flops | bytes accessed | tf_op | source)
XLA Modules:
  0.0 290.1 jit_solution(7245855886508990009)
XLA Ops:
  15.4 5.6 %collective-permute-start.1 = (f32[2,4,4,1024]{3,2,1,0:T(4,128)S(1)}, f32[2,4,4,1024]{3,2,1,0:T(4,128)S(1)}, u32[]{:S(2)}, u32[]{:S(2)}) collective-permute-start(f32[2,4,4,1024]{3,2,1,0:T(4,128)S(1)} %get-tuple-element.91), channel_id=1, source_target_pairs={{0,1},{1,2},{2,3},{4,5},{5,6},{6,7},{8,9},{9,10},{10,11},{12,13},{... | collective-permute-start | bytes 393224 | tf_op jit(solution)/shard_map/ppermute | solution.py:17
  21.0 4.3 %all-to-all-start = ((f32[4,2,8,256]{3,2,1,0:T(8,128)}), f32[4,2,8,256]{3,2,1,0:T(8,128)S(1)}, u32[]{:S(2)}, u32[]{:S(2)}) async-start(f32[4,2,8,256]{3,2,1,0:T(8,128)} %bitcast.10), calls=%async_computation | async-start | bytes 131072 | tf_op jit(solution)/shard_map/all_to_all | solution.py:102
  26.1 4.9 %all-to-all-done = f32[4,2,8,256]{3,2,1,0:T(8,128)S(1)} async-done(((f32[4,2,8,256]{3,2,1,0:T(8,128)}), f32[4,2,8,256]{3,2,1,0:T(8,128)S(1)}, u32[]{:S(2)}, u32[]{:S(2)}) %all-to-all-start) | async-done | bytes 65568 | tf_op jit(solution)/shard_map/all_to_all | solution.py:102
  32.2 3.3 %all-to-all-start.1 = ((f32[1,2,32,256]{3,1,0,2:T(2,128)}), f32[1,2,32,256]{3,1,0,2:T(2,128)S(1)}, u32[]{:S(2)}, u32[]{:S(2)}) async-start(f32[1,2,32,256]{3,1,0,2:T(2,128)} %copy.19), calls=%async_computation.1 | async-start | bytes 131072 | tf_op jit(solution)/shard_map/all_to_all | solution.py:112
  36.2 2.5 fusion.52
  40.8 5.2 %collective-permute-start.3 = (f32[2,4,4,1024]{3,2,1,0:T(4,128)}, f32[2,4,4,1024]{3,2,1,0:T(4,128)}, u32[]{:S(2)}, u32[]{:S(2)}) collective-permute-start(f32[2,4,4,1024]{3,2,1,0:T(4,128)} %get-tuple-element.89), channel_id=1, source_target_pairs={{0,1},{1,2},{2,3},{4,5},{5,6},{6,7},{8,9},{9,10},{10,11},{12,13},{... | collective-permute-start | bytes 393224 | tf_op jit(solution)/shard_map/ppermute | solution.py:17
  48.2 2.5 fusion.36
  59.2 1.7 fusion.110
  63.2 2.7 fusion.64
  65.9 37.3 %reduce-scatter.3.cloned.1.call-done = f32[4,32,128]{2,1,0:T(8,128)} async-done(((f32[4,32,1024]{2,1,0:T(8,128)}), f32[4,32,128]{2,1,0:T(8,128)}) %reduce-scatter.3.cloned.1.call-update) | async-done | bytes 65552 | tf_op jit(solution)/shard_map/reduce_scatter | solution.py:117
  103.2 1.5 multiply_reduce_fusion.2
  104.7 39.5 %all-reduce.1 = (f32[]{:T(128)}, f32[]{:T(128)}) all-reduce(f32[]{:T(128)} %get-tuple-element.3, f32[]{:T(128)} %get-tuple-element.2), channel_id=1, replica_groups=mesh['mem'=8,'tile'=4] {'mem','tile'}, use_global_device_ids=true, to_apply=%region_1.0 | all-reduce | flops 2 | bytes 16 | tf_op jit(solution)/shard_map/psum | solution.py:91
  146.4 12.1 %all_gather.3 = f32[4,32,1024]{2,1,0:T(8,128)S(1)} all-gather(f32[4,32,128]{2,1,0:T(8,128)S(1)} %multiply_subtract_fusion.1), channel_id=1, replica_groups=mesh['mem'=8,'tile'=4] {'mem'}, dimensions={2}, use_global_device_ids=true | all-gather | bytes 589824 | tf_op jit(solution)/shard_map/all_gather | solution.py:125
  159.6 1.4 fusion.108
  163.3 3.8 %all-to-all-start.2 = ((f32[4,2,8,256]{3,2,1,0:T(8,128)}), f32[4,2,8,256]{3,2,1,0:T(8,128)S(1)}, u32[]{:S(2)}, u32[]{:S(2)}) async-start(f32[4,2,8,256]{3,2,1,0:T(8,128)} %bitcast.23), calls=%async_computation.3 | async-start | bytes 131072 | tf_op jit(solution)/shard_map/all_to_all | solution.py:102
  168.4 4.6 %collective-permute-start.5 = (f32[2,4,4,1024]{3,2,1,0:T(4,128)S(1)}, f32[2,4,4,1024]{3,2,1,0:T(4,128)S(1)}, u32[]{:S(2)}, u32[]{:S(2)}) collective-permute-start(f32[2,4,4,1024]{3,2,1,0:T(4,128)S(1)} %get-tuple-element.55), channel_id=1, source_target_pairs={{0,1},{1,2},{2,3},{4,5},{5,6},{6,7},{8,9},{9,10},{10,11},{12,13},{... | collective-permute-start | bytes 393224 | tf_op jit(solution)/shard_map/ppermute | solution.py:17
  174.2 4.2 %all-to-all-start.3 = ((f32[1,2,32,256]{3,1,0,2:T(2,128)}), f32[1,2,32,256]{3,1,0,2:T(2,128)S(1)}, u32[]{:S(2)}, u32[]{:S(2)}) async-start(f32[1,2,32,256]{3,1,0,2:T(2,128)} %copy.22), calls=%async_computation.4 | async-start | bytes 131072 | tf_op jit(solution)/shard_map/all_to_all | solution.py:112
  181.7 4.6 %collective-permute-start.7 = (f32[2,4,4,1024]{3,2,1,0:T(4,128)S(1)}, f32[2,4,4,1024]{3,2,1,0:T(4,128)S(1)}, u32[]{:S(2)}, u32[]{:S(2)}) collective-permute-start(f32[2,4,4,1024]{3,2,1,0:T(4,128)S(1)} %get-tuple-element.53), channel_id=1, source_target_pairs={{0,1},{1,2},{2,3},{4,5},{5,6},{6,7},{8,9},{9,10},{10,11},{12,13},{... | collective-permute-start | bytes 393224 | tf_op jit(solution)/shard_map/ppermute | solution.py:17
  195.5 1.4 fusion.102
  200.9 2.8 fusion.65
  203.7 35.6 %reduce-scatter.5.cloned.1.call-done = f32[4,32,128]{2,1,0:T(8,128)} async-done(((f32[4,32,1024]{2,1,0:T(8,128)}), f32[4,32,128]{2,1,0:T(8,128)}) %reduce-scatter.5.cloned.1.call-update) | async-done | bytes 65552 | tf_op jit(solution)/shard_map/reduce_scatter | solution.py:117
  239.3 1.5 multiply_reduce_fusion
  240.8 39.5 %all-reduce = (f32[]{:T(128)}, f32[]{:T(128)}) all-reduce(f32[]{:T(128)} %get-tuple-element.5, f32[]{:T(128)} %get-tuple-element.4), channel_id=1, replica_groups=mesh['mem'=8,'tile'=4] {'mem','tile'}, use_global_device_ids=true, to_apply=%region_10.11 | all-reduce | flops 2 | bytes 16 | tf_op jit(solution)/shard_map/psum | solution.py:124
  281.7 1.5 multiply_subtract_fusion
  (125 shorter events, 48.5 us)
Async XLA Ops:
  7.2 24.1 %copy-start = (f32[256,256]{1,0:T(8,128)S(1)}, f32[256,256]{1,0:T(8,128)}, u32[]{:S(2)}) copy-start(f32[256,256]{1,0:T(8,128)} %param.9) | copy-start | bytes 786436
  12.6 1.0 copy-start.2
  12.6 1.2 copy-start.3
  13.8 11.5 %copy-start.7 = (f32[2,4,5]{2,1,0:T(4,128)S(1)}, f32[2,4,5]{2,1,0:T(4,128)}, u32[]{:S(2)}) copy-start(f32[2,4,5]{2,1,0:T(4,128)} %param.7) | copy-start | bytes 484
  13.8 17.3 %copy-start.6 = (f32[32,32]{1,0:T(8,128)S(1)}, f32[32,32]{1,0:T(8,128)}, u32[]{:S(2)}) copy-start(f32[32,32]{1,0:T(8,128)} %param.8) | copy-start | bytes 12292
  14.1 21.5 %collective-permute-start = (f32[2,4,4,1024]{3,2,1,0:T(4,128)S(1)}, f32[2,4,4,1024]{3,2,1,0:T(4,128)S(1)}, u32[]{:S(2)}, u32[]{:S(2)}) collective-permute-start(f32[2,4,4,1024]{3,2,1,0:T(4,128)S(1)} %get-tuple-element.90), channel_id=1, source_target_pairs={{1,0},{2,1},{3,2},{5,4},{6,5},{7,6},{9,8},{10,9},{11,10},{13,12},{... | collective-permute-start | bytes 393224 | tf_op jit(solution)/shard_map/ppermute | solution.py:18
  15.4 20.2 %collective-permute-start.1 = (f32[2,4,4,1024]{3,2,1,0:T(4,128)S(1)}, f32[2,4,4,1024]{3,2,1,0:T(4,128)S(1)}, u32[]{:S(2)}, u32[]{:S(2)}) collective-permute-start(f32[2,4,4,1024]{3,2,1,0:T(4,128)S(1)} %get-tuple-element.91), channel_id=1, source_target_pairs={{0,1},{1,2},{2,3},{4,5},{5,6},{6,7},{8,9},{9,10},{10,11},{12,13},{... | collective-permute-start | bytes 393224 | tf_op jit(solution)/shard_map/ppermute | solution.py:17
  21.0 10.1 %all-to-all-start = ((f32[4,2,8,256]{3,2,1,0:T(8,128)}), f32[4,2,8,256]{3,2,1,0:T(8,128)S(1)}, u32[]{:S(2)}, u32[]{:S(2)}) async-start(f32[4,2,8,256]{3,2,1,0:T(8,128)} %bitcast.10), calls=%async_computation | async-start | bytes 131072 | tf_op jit(solution)/shard_map/all_to_all | solution.py:102
  32.2 13.9 %all-to-all-start.1 = ((f32[1,2,32,256]{3,1,0,2:T(2,128)}), f32[1,2,32,256]{3,1,0,2:T(2,128)S(1)}, u32[]{:S(2)}, u32[]{:S(2)}) async-start(f32[1,2,32,256]{3,1,0,2:T(2,128)} %copy.19), calls=%async_computation.1 | async-start | bytes 131072 | tf_op jit(solution)/shard_map/all_to_all | solution.py:112
  35.5 67.7 %reduce-scatter.3.cloned.1.call-start = ((), (), s32[]{:S(2)}) async-start(), calls=%async_computation.6 | async-start | bytes 589824 | tf_op jit(solution)/shard_map/reduce_scatter | solution.py:117
  35.5 0.7 copy-start.4
  35.6 0.7 copy-start.5
  39.5 8.7 %collective-permute-start.2 = (f32[2,4,4,1024]{3,2,1,0:T(4,128)}, f32[2,4,4,1024]{3,2,1,0:T(4,128)}, u32[]{:S(2)}, u32[]{:S(2)}) collective-permute-start(f32[2,4,4,1024]{3,2,1,0:T(4,128)} %get-tuple-element.88), channel_id=1, source_target_pairs={{1,0},{2,1},{3,2},{5,4},{6,5},{7,6},{9,8},{10,9},{11,10},{13,12},{... | collective-permute-start | bytes 393224 | tf_op jit(solution)/shard_map/ppermute | solution.py:18
  40.8 7.4 %collective-permute-start.3 = (f32[2,4,4,1024]{3,2,1,0:T(4,128)}, f32[2,4,4,1024]{3,2,1,0:T(4,128)}, u32[]{:S(2)}, u32[]{:S(2)}) collective-permute-start(f32[2,4,4,1024]{3,2,1,0:T(4,128)} %get-tuple-element.89), channel_id=1, source_target_pairs={{0,1},{1,2},{2,3},{4,5},{5,6},{6,7},{8,9},{9,10},{10,11},{12,13},{... | collective-permute-start | bytes 393224 | tf_op jit(solution)/shard_map/ppermute | solution.py:17
  163.3 9.8 %all-to-all-start.2 = ((f32[4,2,8,256]{3,2,1,0:T(8,128)}), f32[4,2,8,256]{3,2,1,0:T(8,128)S(1)}, u32[]{:S(2)}, u32[]{:S(2)}) async-start(f32[4,2,8,256]{3,2,1,0:T(8,128)} %bitcast.23), calls=%async_computation.3 | async-start | bytes 131072 | tf_op jit(solution)/shard_map/all_to_all | solution.py:102
  167.1 11.2 %collective-permute-start.4 = (f32[2,4,4,1024]{3,2,1,0:T(4,128)S(1)}, f32[2,4,4,1024]{3,2,1,0:T(4,128)S(1)}, u32[]{:S(2)}, u32[]{:S(2)}) collective-permute-start(f32[2,4,4,1024]{3,2,1,0:T(4,128)S(1)} %get-tuple-element.54), channel_id=1, source_target_pairs={{1,0},{2,1},{3,2},{5,4},{6,5},{7,6},{9,8},{10,9},{11,10},{13,12},{... | collective-permute-start | bytes 393224 | tf_op jit(solution)/shard_map/ppermute | solution.py:18
  168.4 9.9 %collective-permute-start.5 = (f32[2,4,4,1024]{3,2,1,0:T(4,128)S(1)}, f32[2,4,4,1024]{3,2,1,0:T(4,128)S(1)}, u32[]{:S(2)}, u32[]{:S(2)}) collective-permute-start(f32[2,4,4,1024]{3,2,1,0:T(4,128)S(1)} %get-tuple-element.55), channel_id=1, source_target_pairs={{0,1},{1,2},{2,3},{4,5},{5,6},{6,7},{8,9},{9,10},{10,11},{12,13},{... | collective-permute-start | bytes 393224 | tf_op jit(solution)/shard_map/ppermute | solution.py:17
  174.2 12.1 %all-to-all-start.3 = ((f32[1,2,32,256]{3,1,0,2:T(2,128)}), f32[1,2,32,256]{3,1,0,2:T(2,128)S(1)}, u32[]{:S(2)}, u32[]{:S(2)}) async-start(f32[1,2,32,256]{3,1,0,2:T(2,128)} %copy.22), calls=%async_computation.4 | async-start | bytes 131072 | tf_op jit(solution)/shard_map/all_to_all | solution.py:112
  178.4 61.0 %reduce-scatter.5.cloned.1.call-start = ((), (), s32[]{:S(2)}) async-start(), calls=%async_computation.7 | async-start | bytes 589824 | tf_op jit(solution)/shard_map/reduce_scatter | solution.py:117
  180.4 8.0 %collective-permute-start.6 = (f32[2,4,4,1024]{3,2,1,0:T(4,128)}, f32[2,4,4,1024]{3,2,1,0:T(4,128)S(1)}, u32[]{:S(2)}, u32[]{:S(2)}) collective-permute-start(f32[2,4,4,1024]{3,2,1,0:T(4,128)} %get-tuple-element.52), channel_id=1, source_target_pairs={{1,0},{2,1},{3,2},{5,4},{6,5},{7,6},{9,8},{10,9},{11,10},{13,12},{... | collective-permute-start | bytes 393224 | tf_op jit(solution)/shard_map/ppermute | solution.py:18
  181.7 7.1 %collective-permute-start.7 = (f32[2,4,4,1024]{3,2,1,0:T(4,128)S(1)}, f32[2,4,4,1024]{3,2,1,0:T(4,128)S(1)}, u32[]{:S(2)}, u32[]{:S(2)}) collective-permute-start(f32[2,4,4,1024]{3,2,1,0:T(4,128)S(1)} %get-tuple-element.53), channel_id=1, source_target_pairs={{0,1},{1,2},{2,3},{4,5},{5,6},{6,7},{8,9},{9,10},{10,11},{12,13},{... | collective-permute-start | bytes 393224 | tf_op jit(solution)/shard_map/ppermute | solution.py:17
  200.9 82.3 %copy-start.1 = (f32[256,256]{1,0:T(8,128)S(1)}, f32[256,256]{1,0:T(8,128)}, u32[]{:S(2)}) copy-start(f32[256,256]{1,0:T(8,128)} %param.9) | copy-start | bytes 786436
Sparse Core Ops, SparseCore 0:
  66.1 37.0 reduce-scatter.2
  203.9 35.4 reduce-scatter.4
where the time goes:
time: 291 us; the launch traced here: 290 us
  blocking collectives  91.2 us (31%)
  waiting for transfers between devices  78.2 us (27%)
  starting transfers between devices  40.7 us (14%)
  other arithmetic  29.8 us (10%)
  local copies, waits for them, and re-layouts  21.9 us (8%)
  between operations  17.4 us (6%)
  matrix products  11 us (4%)
    psum x2, blocking collectives, local(): squares = lax.psum(jnp.sum(residual * residual), ('mem', 'tile'))  79.1 us
    reduce_scatter x2, waiting for transfers between devices, local(): lax.psum_scatter(partial_value, 'mem', scatter_dimension=2, tiled=True)  72.9 us
    ppermute x4, starting transfers between devices, extended_2(): before = lax.ppermute(last, axis, up)  19.9 us
    all_gather x1, blocking collectives, local(): residual_full = lax.all_gather(residual, 'mem', axis=2, tiled=True)  12.1 us
    all_to_all x2, starting transfers between devices, local(): lax.all_to_all(coarse_items, 'tile', split_axis=0, concat_axis=2, tiled=T...  8.15 us
    add x4, other arithmetic, lat_valid(): result + kernel[None, :, offset, None, None] * (values[:, :, 4 + offset:4...  7.76 us
    slice x32, local copies, waits for them, and re-layouts, lon_pass(): jnp.roll(values, -offset, axis=3)  7.69 us
    all_to_all x2, starting transfers between devices, local(): lax.all_to_all(smoothed, 'tile', split_axis=2, concat_axis=0, tiled=True)  7.47 us
  transfers between devices with their start and end apart: 14, of which 4 were waited for; matrix products, arithmetic and copies ran while one was open for 4% of the time, Pallas kernels for 0%

commit v1 on v0

--- a/solution.py
+++ b/solution.py
@@ -109,8 +109,11 @@
             detail = lat_valid(extended, kernel[0], height)
         apply_detail = detail
         apply_detail = lon_pass(lon_pass(apply_detail, kernel[1]), kernel[1])
-        returned = lax.all_to_all(
-            smoothed, "tile", split_axis=2, concat_axis=0, tiled=True
+        returned = jnp.concatenate(
+            lax.all_to_all(
+                jnp.stack(jnp.split(smoothed, lax.axis_size("tile"), axis=2)), "tile", 0, 0
+            ),
+            axis=0,
         ).reshape(count_local, levels, height // 4, extent // 4)
         blended = apply_detail - prolong(block_mean(apply_detail)) + prolong(returned)
         partial_value = jnp.sum(perturbations.astype(jnp.float32) * blended, axis=0)

time: 291 us -> 291 us (level)
  no operation moved by 1% of the time
where the time goes in v1:
time: 291 us; the launch traced here: 290 us
  blocking collectives  91.1 us (31%)
  waiting for transfers between devices  78.3 us (27%)
  starting transfers between devices  40.7 us (14%)
  other arithmetic  31.1 us (11%)
  local copies, waits for them, and re-layouts  20.4 us (7%)
  between operations  17.4 us (6%)
  matrix products  11 us (4%)
    psum x2, blocking collectives, local(): squares = lax.psum(jnp.sum(residual * residual), ('mem', 'tile'))  79 us
    reduce_scatter x2, waiting for transfers between devices, local(): lax.psum_scatter(partial_value, 'mem', scatter_dimension=2, tiled=True)  72.9 us
    ppermute x4, starting transfers between devices, extended_2(): before = lax.ppermute(last, axis, up)  19.9 us
    all_gather x1, blocking collectives, local(): residual_full = lax.all_gather(residual, 'mem', axis=2, tiled=True)  12.1 us
    all_to_all x2, starting transfers between devices, local(): lax.all_to_all(coarse_items, 'tile', split_axis=0, concat_axis=2, tiled=T...  8.15 us
    add x4, other arithmetic, lat_valid(): result + kernel[None, :, offset, None, None] * (values[:, :, 4 + offset:4...  7.84 us
    slice x32, local copies, waits for them, and re-layouts, lon_pass(): jnp.roll(values, -offset, axis=3)  7.69 us
    all_to_all x2, starting transfers between devices, local(): lax.all_to_all(jnp.stack(jnp.split(smoothed, lax.axis_size('tile'), axis=...  7.47 us
  transfers between devices with their start and end apart: 14, of which 4 were waited for; matrix products, arithmetic and copies ran while one was open for 4% of the time, Pallas kernels for 0%

profile of v1, /device:TPU:0, one launch (start us, length us, event | category | flops | bytes accessed | tf_op | source)
XLA Modules:
  0.0 290.0 jit_solution(13487958482676459193)
XLA Ops:
  9.5 1.4 fusion.112
  15.4 5.6 %collective-permute-start.1 = (f32[2,4,4,1024]{3,2,1,0:T(4,128)S(1)}, f32[2,4,4,1024]{3,2,1,0:T(4,128)S(1)}, u32[]{:S(2)}, u32[]{:S(2)}) collective-permute-start(f32[2,4,4,1024]{3,2,1,0:T(4,128)S(1)} %get-tuple-element.91), channel_id=1, source_target_pairs={{0,1},{1,2},{2,3},{4,5},{5,6},{6,7},{8,9},{9,10},{10,11},{12,13},{... | collective-permute-start | bytes 393224 | tf_op jit(solution)/shard_map/ppermute | solution.py:17
  21.0 4.3 %all-to-all-start = ((f32[4,2,8,256]{3,2,1,0:T(8,128)}), f32[4,2,8,256]{3,2,1,0:T(8,128)S(1)}, u32[]{:S(2)}, u32[]{:S(2)}) async-start(f32[4,2,8,256]{3,2,1,0:T(8,128)} %bitcast.10), calls=%async_computation | async-start | bytes 131072 | tf_op jit(solution)/shard_map/all_to_all | solution.py:102
  26.1 4.9 %all-to-all-done = f32[4,2,8,256]{3,2,1,0:T(8,128)S(1)} async-done(((f32[4,2,8,256]{3,2,1,0:T(8,128)}), f32[4,2,8,256]{3,2,1,0:T(8,128)S(1)}, u32[]{:S(2)}, u32[]{:S(2)}) %all-to-all-start) | async-done | bytes 65568 | tf_op jit(solution)/shard_map/all_to_all | solution.py:102
  32.2 3.3 %all-to-all-start.1 = ((f32[4,1,2,8,256]{4,3,2,1,0:T(8,128)}), f32[4,1,2,8,256]{4,3,2,1,0:T(8,128)S(1)}, u32[]{:S(2)}, u32[]{:S(2)}) async-start(f32[4,1,2,8,256]{4,3,2,1,0:T(8,128)} %pad_maximum_fusion.8), calls=%async_computation.1 | async-start | bytes 131072 | tf_op jit(solution)/shard_map/all_to_all | solution.py:113
  36.2 2.5 fusion.52
  40.8 5.2 %collective-permute-start.3 = (f32[2,4,4,1024]{3,2,1,0:T(4,128)}, f32[2,4,4,1024]{3,2,1,0:T(4,128)}, u32[]{:S(2)}, u32[]{:S(2)}) collective-permute-start(f32[2,4,4,1024]{3,2,1,0:T(4,128)} %get-tuple-element.89), channel_id=1, source_target_pairs={{0,1},{1,2},{2,3},{4,5},{5,6},{6,7},{8,9},{9,10},{10,11},{12,13},{... | collective-permute-start | bytes 393224 | tf_op jit(solution)/shard_map/ppermute | solution.py:17
  48.2 2.6 fusion.36
  59.3 1.7 fusion.110
  63.2 2.7 fusion.64
  66.0 37.3 %reduce-scatter.3.cloned.1.call-done = f32[4,32,128]{2,1,0:T(8,128)} async-done(((f32[4,32,1024]{2,1,0:T(8,128)}), f32[4,32,128]{2,1,0:T(8,128)}) %reduce-scatter.3.cloned.1.call-update) | async-done | bytes 65552 | tf_op jit(solution)/shard_map/reduce_scatter | solution.py:120
  103.3 1.5 multiply_reduce_fusion.2
  104.7 39.5 %all-reduce.1 = (f32[]{:T(128)}, f32[]{:T(128)}) all-reduce(f32[]{:T(128)} %get-tuple-element.3, f32[]{:T(128)} %get-tuple-element.2), channel_id=1, replica_groups=mesh['mem'=8,'tile'=4] {'mem','tile'}, use_global_device_ids=true, to_apply=%region_1.0 | all-reduce | flops 2 | bytes 16 | tf_op jit(solution)/shard_map/psum | solution.py:91
  146.4 12.1 %all_gather.3 = f32[4,32,1024]{2,1,0:T(8,128)S(1)} all-gather(f32[4,32,128]{2,1,0:T(8,128)S(1)} %multiply_subtract_fusion.1), channel_id=1, replica_groups=mesh['mem'=8,'tile'=4] {'mem'}, dimensions={2}, use_global_device_ids=true | all-gather | bytes 589824 | tf_op jit(solution)/shard_map/all_gather | solution.py:128
  163.3 3.8 %all-to-all-start.2 = ((f32[4,2,8,256]{3,2,1,0:T(8,128)}), f32[4,2,8,256]{3,2,1,0:T(8,128)S(1)}, u32[]{:S(2)}, u32[]{:S(2)}) async-start(f32[4,2,8,256]{3,2,1,0:T(8,128)} %bitcast.25), calls=%async_computation.3 | async-start | bytes 131072 | tf_op jit(solution)/shard_map/all_to_all | solution.py:102
  168.5 4.6 %collective-permute-start.5 = (f32[2,4,4,1024]{3,2,1,0:T(4,128)S(1)}, f32[2,4,4,1024]{3,2,1,0:T(4,128)S(1)}, u32[]{:S(2)}, u32[]{:S(2)}) collective-permute-start(f32[2,4,4,1024]{3,2,1,0:T(4,128)S(1)} %get-tuple-element.55), channel_id=1, source_target_pairs={{0,1},{1,2},{2,3},{4,5},{5,6},{6,7},{8,9},{9,10},{10,11},{12,13},{... | collective-permute-start | bytes 393224 | tf_op jit(solution)/shard_map/ppermute | solution.py:17
  174.2 4.2 %all-to-all-start.3 = ((f32[4,1,2,8,256]{4,3,2,1,0:T(8,128)}), f32[4,1,2,8,256]{4,3,2,1,0:T(8,128)S(1)}, u32[]{:S(2)}, u32[]{:S(2)}) async-start(f32[4,1,2,8,256]{4,3,2,1,0:T(8,128)} %pad_maximum_fusion.9), calls=%async_computation.4 | async-start | bytes 131072 | tf_op jit(solution)/shard_map/all_to_all | solution.py:113
  181.7 4.6 %collective-permute-start.7 = (f32[2,4,4,1024]{3,2,1,0:T(4,128)S(1)}, f32[2,4,4,1024]{3,2,1,0:T(4,128)S(1)}, u32[]{:S(2)}, u32[]{:S(2)}) collective-permute-start(f32[2,4,4,1024]{3,2,1,0:T(4,128)S(1)} %get-tuple-element.53), channel_id=1, source_target_pairs={{0,1},{1,2},{2,3},{4,5},{5,6},{6,7},{8,9},{9,10},{10,11},{12,13},{... | collective-permute-start | bytes 393224 | tf_op jit(solution)/shard_map/ppermute | solution.py:17
  195.5 1.4 fusion.102
  200.9 2.8 fusion.65
  203.7 35.6 %reduce-scatter.5.cloned.1.call-done = f32[4,32,128]{2,1,0:T(8,128)} async-done(((f32[4,32,1024]{2,1,0:T(8,128)}), f32[4,32,128]{2,1,0:T(8,128)}) %reduce-scatter.5.cloned.1.call-update) | async-done | bytes 65552 | tf_op jit(solution)/shard_map/reduce_scatter | solution.py:120
  239.3 1.5 multiply_reduce_fusion
  240.8 39.5 %all-reduce = (f32[]{:T(128)}, f32[]{:T(128)}) all-reduce(f32[]{:T(128)} %get-tuple-element.5, f32[]{:T(128)} %get-tuple-element.4), channel_id=1, replica_groups=mesh['mem'=8,'tile'=4] {'mem','tile'}, use_global_device_ids=true, to_apply=%region_10.11 | all-reduce | flops 2 | bytes 16 | tf_op jit(solution)/shard_map/psum | solution.py:127
  281.6 1.5 multiply_subtract_fusion
  (125 shorter events, 48.4 us)
Async XLA Ops:
  7.2 24.1 %copy-start = (f32[256,256]{1,0:T(8,128)S(1)}, f32[256,256]{1,0:T(8,128)}, u32[]{:S(2)}) copy-start(f32[256,256]{1,0:T(8,128)} %param.9) | copy-start | bytes 786436
  12.6 1.0 copy-start.2
  12.6 1.2 copy-start.3
  13.8 11.5 %copy-start.7 = (f32[2,4,5]{2,1,0:T(4,128)S(1)}, f32[2,4,5]{2,1,0:T(4,128)}, u32[]{:S(2)}) copy-start(f32[2,4,5]{2,1,0:T(4,128)} %param.7) | copy-start | bytes 484
  13.8 17.3 %copy-start.6 = (f32[32,32]{1,0:T(8,128)S(1)}, f32[32,32]{1,0:T(8,128)}, u32[]{:S(2)}) copy-start(f32[32,32]{1,0:T(8,128)} %param.8) | copy-start | bytes 12292
  14.1 21.4 %collective-permute-start = (f32[2,4,4,1024]{3,2,1,0:T(4,128)S(1)}, f32[2,4,4,1024]{3,2,1,0:T(4,128)S(1)}, u32[]{:S(2)}, u32[]{:S(2)}) collective-permute-start(f32[2,4,4,1024]{3,2,1,0:T(4,128)S(1)} %get-tuple-element.90), channel_id=1, source_target_pairs={{1,0},{2,1},{3,2},{5,4},{6,5},{7,6},{9,8},{10,9},{11,10},{13,12},{... | collective-permute-start | bytes 393224 | tf_op jit(solution)/shard_map/ppermute | solution.py:18
  15.4 20.1 %collective-permute-start.1 = (f32[2,4,4,1024]{3,2,1,0:T(4,128)S(1)}, f32[2,4,4,1024]{3,2,1,0:T(4,128)S(1)}, u32[]{:S(2)}, u32[]{:S(2)}) collective-permute-start(f32[2,4,4,1024]{3,2,1,0:T(4,128)S(1)} %get-tuple-element.91), channel_id=1, source_target_pairs={{0,1},{1,2},{2,3},{4,5},{5,6},{6,7},{8,9},{9,10},{10,11},{12,13},{... | collective-permute-start | bytes 393224 | tf_op jit(solution)/shard_map/ppermute | solution.py:17
  21.0 10.1 %all-to-all-start = ((f32[4,2,8,256]{3,2,1,0:T(8,128)}), f32[4,2,8,256]{3,2,1,0:T(8,128)S(1)}, u32[]{:S(2)}, u32[]{:S(2)}) async-start(f32[4,2,8,256]{3,2,1,0:T(8,128)} %bitcast.10), calls=%async_computation | async-start | bytes 131072 | tf_op jit(solution)/shard_map/all_to_all | solution.py:102
  32.2 13.9 %all-to-all-start.1 = ((f32[4,1,2,8,256]{4,3,2,1,0:T(8,128)}), f32[4,1,2,8,256]{4,3,2,1,0:T(8,128)S(1)}, u32[]{:S(2)}, u32[]{:S(2)}) async-start(f32[4,1,2,8,256]{4,3,2,1,0:T(8,128)} %pad_maximum_fusion.8), calls=%async_computation.1 | async-start | bytes 131072 | tf_op jit(solution)/shard_map/all_to_all | solution.py:113
  35.4 67.8 %reduce-scatter.3.cloned.1.call-start = ((), (), s32[]{:S(2)}) async-start(), calls=%async_computation.6 | async-start | bytes 589824 | tf_op jit(solution)/shard_map/reduce_scatter | solution.py:120
  35.5 0.6 copy-start.4
  35.5 0.7 copy-start.5
  39.5 8.6 %collective-permute-start.2 = (f32[2,4,4,1024]{3,2,1,0:T(4,128)}, f32[2,4,4,1024]{3,2,1,0:T(4,128)}, u32[]{:S(2)}, u32[]{:S(2)}) collective-permute-start(f32[2,4,4,1024]{3,2,1,0:T(4,128)} %get-tuple-element.88), channel_id=1, source_target_pairs={{1,0},{2,1},{3,2},{5,4},{6,5},{7,6},{9,8},{10,9},{11,10},{13,12},{... | collective-permute-start | bytes 393224 | tf_op jit(solution)/shard_map/ppermute | solution.py:18
  40.8 7.4 %collective-permute-start.3 = (f32[2,4,4,1024]{3,2,1,0:T(4,128)}, f32[2,4,4,1024]{3,2,1,0:T(4,128)}, u32[]{:S(2)}, u32[]{:S(2)}) collective-permute-start(f32[2,4,4,1024]{3,2,1,0:T(4,128)} %get-tuple-element.89), channel_id=1, source_target_pairs={{0,1},{1,2},{2,3},{4,5},{5,6},{6,7},{8,9},{9,10},{10,11},{12,13},{... | collective-permute-start | bytes 393224 | tf_op jit(solution)/shard_map/ppermute | solution.py:17
  163.3 9.8 %all-to-all-start.2 = ((f32[4,2,8,256]{3,2,1,0:T(8,128)}), f32[4,2,8,256]{3,2,1,0:T(8,128)S(1)}, u32[]{:S(2)}, u32[]{:S(2)}) async-start(f32[4,2,8,256]{3,2,1,0:T(8,128)} %bitcast.25), calls=%async_computation.3 | async-start | bytes 131072 | tf_op jit(solution)/shard_map/all_to_all | solution.py:102
  167.2 11.2 %collective-permute-start.4 = (f32[2,4,4,1024]{3,2,1,0:T(4,128)S(1)}, f32[2,4,4,1024]{3,2,1,0:T(4,128)S(1)}, u32[]{:S(2)}, u32[]{:S(2)}) collective-permute-start(f32[2,4,4,1024]{3,2,1,0:T(4,128)S(1)} %get-tuple-element.54), channel_id=1, source_target_pairs={{1,0},{2,1},{3,2},{5,4},{6,5},{7,6},{9,8},{10,9},{11,10},{13,12},{... | collective-permute-start | bytes 393224 | tf_op jit(solution)/shard_map/ppermute | solution.py:18
  168.5 9.9 %collective-permute-start.5 = (f32[2,4,4,1024]{3,2,1,0:T(4,128)S(1)}, f32[2,4,4,1024]{3,2,1,0:T(4,128)S(1)}, u32[]{:S(2)}, u32[]{:S(2)}) collective-permute-start(f32[2,4,4,1024]{3,2,1,0:T(4,128)S(1)} %get-tuple-element.55), channel_id=1, source_target_pairs={{0,1},{1,2},{2,3},{4,5},{5,6},{6,7},{8,9},{9,10},{10,11},{12,13},{... | collective-permute-start | bytes 393224 | tf_op jit(solution)/shard_map/ppermute | solution.py:17
  174.2 12.1 %all-to-all-start.3 = ((f32[4,1,2,8,256]{4,3,2,1,0:T(8,128)}), f32[4,1,2,8,256]{4,3,2,1,0:T(8,128)S(1)}, u32[]{:S(2)}, u32[]{:S(2)}) async-start(f32[4,1,2,8,256]{4,3,2,1,0:T(8,128)} %pad_maximum_fusion.9), calls=%async_computation.4 | async-start | bytes 131072 | tf_op jit(solution)/shard_map/all_to_all | solution.py:113
  178.4 61.0 %reduce-scatter.5.cloned.1.call-start = ((), (), s32[]{:S(2)}) async-start(), calls=%async_computation.7 | async-start | bytes 589824 | tf_op jit(solution)/shard_map/reduce_scatter | solution.py:120
  180.4 8.0 %collective-permute-start.6 = (f32[2,4,4,1024]{3,2,1,0:T(4,128)}, f32[2,4,4,1024]{3,2,1,0:T(4,128)S(1)}, u32[]{:S(2)}, u32[]{:S(2)}) collective-permute-start(f32[2,4,4,1024]{3,2,1,0:T(4,128)} %get-tuple-element.52), channel_id=1, source_target_pairs={{1,0},{2,1},{3,2},{5,4},{6,5},{7,6},{9,8},{10,9},{11,10},{13,12},{... | collective-permute-start | bytes 393224 | tf_op jit(solution)/shard_map/ppermute | solution.py:18
  181.7 7.1 %collective-permute-start.7 = (f32[2,4,4,1024]{3,2,1,0:T(4,128)S(1)}, f32[2,4,4,1024]{3,2,1,0:T(4,128)S(1)}, u32[]{:S(2)}, u32[]{:S(2)}) collective-permute-start(f32[2,4,4,1024]{3,2,1,0:T(4,128)S(1)} %get-tuple-element.53), channel_id=1, source_target_pairs={{0,1},{1,2},{2,3},{4,5},{5,6},{6,7},{8,9},{9,10},{10,11},{12,13},{... | collective-permute-start | bytes 393224 | tf_op jit(solution)/shard_map/ppermute | solution.py:17
  200.9 82.3 %copy-start.1 = (f32[256,256]{1,0:T(8,128)S(1)}, f32[256,256]{1,0:T(8,128)}, u32[]{:S(2)}) copy-start(f32[256,256]{1,0:T(8,128)} %param.9) | copy-start | bytes 786436
Sparse Core Ops, SparseCore 0:
  66.1 37.1 reduce-scatter.2
  203.8 35.4 reduce-scatter.4
